TPU v7x, 32 devices: a whole 2x2x4 slice. The times are simulated.
32 devices in a mesh: group: 4 (over x, core), seq: 2 (over y), expert: 4 (over z).
Axes of the slice: x: 2, y: 2, z: 4, core: 2. Of those that a mesh axis runs over, the one named last changes fastest.
Arguments:
- queries: bfloat16 [16, 32, 128], P('expert', 'group')
- keys: bfloat16 [16, 256, 8, 128], P('expert', 'seq', 'group')
- values: bfloat16 [16, 256, 8, 128], P('expert', 'seq', 'group'), may hold values from -48 to 48
- block_of_slot: int32 [16, 16], P('expert', 'seq'), may hold values from 0 to 15, each once within a row
- lengths: int32 [16], P('expert'), may hold values from 128 to 256
- out_proj: bfloat16 [4096, 4096], P('group', 'seq'), may hold values from -0.09375 to 0.09375
- residual: bfloat16 [16, 4096], P('expert', 'seq'), may hold values from -6 to 6
- norm_gain: bfloat16 [4096], replicated, may hold values from 0.25 to 1.75
- router: bfloat16 [4096, 8], replicated, may hold values from -0.09375 to 0.09375
- routes: int32 [16, 2], P('expert'), may hold values from 0 to 7, all different within a row; in each aligned block of 4 rows (0 to 3, 4 to 7, ...) at most 2 rows name the same one
- w_gate: bfloat16 [8, 4096, 14336], P('expert', None, ('group', 'seq')), may hold values from -0.09375 to 0.09375
- w_up: bfloat16 [8, 4096, 14336], P('expert', None, ('group', 'seq')), may hold values from -0.09375 to 0.09375
- w_down: bfloat16 [8, 14336, 4096], P('expert', ('group', 'seq')), may hold values from -0.046875 to 0.046875
Outputs:
- layer_out: bfloat16 [16, 4096], P('expert', 'seq')
Inputs may be any that keep to these rules, and one draw needn't show every extreme that they name: `block_of_slot`: each row lists every logical block once. `routes`: the two ids of a row differ; among the 4 rows of one device no expert is named more than 2 times, and in some such blocks one expert is named exactly 2 times.
All inputs are finite; a program needn't handle non-finite values.
Results may differ from a plain program's by a relative error of at most 0.013.
Values may be sent and summed in bfloat16 or wider, within the bound.
No kernel may reach another device: no remote copies, remote signals or barrier semaphores. Data moves between devices by JAX's collectives and lax.ppermute only.
A program may use at most 128 MiB of HBM per device.

v0:
```python
import jax
import jax.numpy as jnp
from jax import lax
from jax.sharding import PartitionSpec as P

BLOCK = 16
CAPACITY = 2
masked_score = -1e30


def combined_all(value, axis, combine):
    everything = jax.tree.map(lambda part: lax.all_gather(part, axis), value)
    initial = jax.tree.map(lambda part: part[0], everything)

    def hop(k, so_far):
        return combine(so_far, jax.tree.map(lambda part: part[k], everything))

    return lax.fori_loop(1, lax.axis_size(axis), hop, initial)


def combine_carry(earlier, later):
    high_a, total_a, sums_a = earlier
    high_b, total_b, sums_b = later
    highest = jnp.maximum(high_a, high_b)
    scale_a = jnp.exp(high_a - highest)
    scale_b = jnp.exp(high_b - highest)
    return (
        highest,
        total_a * scale_a + total_b * scale_b,
        sums_a * scale_a[..., None] + sums_b * scale_b[..., None],
    )


def shards(
    queries,
    keys,
    values,
    block_of_slot,
    lengths,
    out_proj,
    residual,
    norm_gain,
    router,
    routes,
    w_gate,
    w_up,
    w_down,
):
    batch_rows, local_heads, head_dim = queries.shape
    span_len = keys.shape[1]
    kv_local = keys.shape[2]
    per_kv = local_heads // kv_local
    grouped = queries.reshape(batch_rows, kv_local, per_kv, head_dim)
    scores = jnp.einsum(
        "rkgd,rlkd->rkgl", grouped, keys, preferred_element_type=jnp.float32
    ) * head_dim ** (-0.5)
    offsets = jnp.arange(BLOCK, dtype=jnp.int32)
    position = (block_of_slot[:, :, None] * BLOCK + offsets[None, None, :]).reshape(
        batch_rows, span_len
    )
    visible = (position < lengths[:, None])[:, None, None, :]
    masked = jnp.where(visible, scores, masked_score)
    highest = jnp.max(masked, axis=-1)
    probs = jnp.where(visible, jnp.exp(masked - highest[..., None]), 0.0)
    totals = jnp.sum(probs, axis=-1)
    weighted = jnp.einsum(
        "rkgl,rlkd->rkgd", probs.astype(jnp.bfloat16), values, preferred_element_type=jnp.float32
    )
    local_carry = (highest, totals, weighted)
    highest, totals, weighted = combined_all(local_carry, "seq", combine_carry)
    attended = (
        (weighted / totals[..., None])
        .astype(jnp.bfloat16)
        .reshape(batch_rows, local_heads * head_dim)
    )
    partial_value = jnp.dot(attended, out_proj, preferred_element_type=jnp.float32)
    attention = lax.psum(partial_value, "group")
    hidden = residual.astype(jnp.float32) + attention
    full_rows = lax.all_gather(hidden, "seq", axis=1, tiled=True)
    meansq = jnp.mean(full_rows * full_rows, axis=-1, keepdims=True)
    normed = (full_rows * lax.rsqrt(meansq + 1e-05) * norm_gain.astype(jnp.float32)).astype(
        jnp.bfloat16
    )
    logits = jnp.dot(normed, router, preferred_element_type=jnp.float32)
    experts = router.shape[1]
    onehot = (routes[:, :, None] == jnp.arange(experts, dtype=jnp.int32)[None, None, :]).astype(
        jnp.int32
    )
    chosen = jnp.sum(onehot.astype(jnp.float32) * logits[:, None, :], axis=-1)
    gate_probs = jax.nn.softmax(chosen, axis=-1)
    per_row = jnp.sum(onehot, axis=1)
    earlier = jnp.cumsum(per_row, axis=0) - per_row
    slot_index = jnp.sum(onehot * earlier[:, None, :], axis=2)
    in_slot = (
        slot_index[:, :, None] == jnp.arange(CAPACITY, dtype=jnp.int32)[None, None, :]
    ).astype(jnp.int32)
    chart = onehot[:, :, :, None] * in_slot[:, :, None, :]
    picker = jnp.sum(chart, axis=1).astype(jnp.bfloat16)
    outbound = jnp.einsum("rec,rd->ecd", picker, normed, preferred_element_type=jnp.float32).astype(
        jnp.bfloat16
    )
    expert_devs = lax.axis_size("expert")
    local_experts = experts // expert_devs
    model_width = normed.shape[1]
    outbound = outbound.reshape(expert_devs, local_experts, CAPACITY, model_width)
    inbound = lax.all_to_all(outbound, "expert", split_axis=0, concat_axis=0, tiled=True)
    gate_act = jnp.einsum("secd,edf->secf", inbound, w_gate, preferred_element_type=jnp.float32)
    upper = jnp.einsum("secd,edf->secf", inbound, w_up, preferred_element_type=jnp.float32)
    activated = (jax.nn.silu(gate_act) * upper).astype(jnp.bfloat16)
    down_terms = jnp.einsum("secf,efd->secd", activated, w_down, preferred_element_type=jnp.float32)
    summed = lax.psum(down_terms.astype(jnp.bfloat16), ("group", "seq")).astype(jnp.float32)
    col_width = summed.shape[3] // lax.axis_size("seq")
    my_cols = lax.dynamic_slice_in_dim(summed, lax.axis_index("seq") * col_width, col_width, 3)
    returned = lax.all_to_all(
        my_cols.astype(jnp.bfloat16), "expert", split_axis=0, concat_axis=0, tiled=True
    )
    returned = returned.reshape(experts, CAPACITY, returned.shape[3]).astype(jnp.float32)
    mixing = jnp.sum(gate_probs[:, :, None, None] * chart.astype(jnp.float32), axis=1)
    expert_mix = jnp.einsum("rec,ecd->rd", mixing, returned, precision=lax.Precision.HIGHEST)
    return (hidden + expert_mix).astype(jnp.bfloat16)


def solution(mesh):
    return jax.shard_map(
        shards,
        mesh=mesh,
        in_specs=(
            P("expert", "group", None),
            P("expert", "seq", "group", None),
            P("expert", "seq", "group", None),
            P("expert", "seq"),
            P("expert"),
            P("group", "seq"),
            P("expert", "seq"),
            P(),
            P(),
            P("expert", None),
            P("expert", None, ("group", "seq")),
            P("expert", None, ("group", "seq")),
            P("expert", ("group", "seq"), None),
        ),
        out_specs=P("expert", "seq"),
        check_vma=False,
    )
```

profile of v0, /device:TPU:0, one launch (start us, length us, event | category | flops | bytes accessed | tf_op | source)
XLA Modules:
  0.0 164.8 jit_solution(3506737250032493510)
XLA Ops:
  6.5 0.0 copy-start
  6.5 0.8 fusion.56
  7.3 0.7 fusion.55
  8.1 0.7 broadcast_multiply_fusion
  8.8 0.1 add.70
  8.8 0.1 add.71
  8.9 0.1 add.73
  9.0 0.7 add_compare_fusion
  9.8 0.0 copy-done
  9.8 1.0 fusion.64
  10.8 5.3 %all-gather.1 = f32[8,2,4]{2,1,0:T(2,128)S(1)} all-gather(f32[4,2,4]{2,1,0:T(2,128)S(1)} %get-tuple-element.22), channel_id=3, replica_groups=mesh['group'=4,'seq'=2,'expert'=4] {'seq'}, dimensions={0}, use_global_device_ids=true | all-gather | bytes 384 | tf_op jit(solution)/shard_map/all_gather | solution.py:12
  16.1 0.2 fusion.44
  16.3 1.2 fusion.29
  17.4 4.4 %all-gather = f32[8,2,4,128]{3,2,1,0:T(4,128)S(1)} all-gather(f32[4,2,4,128]{3,2,1,0:T(4,128)S(1)} %fusion.29), channel_id=2, replica_groups=mesh['group'=4,'seq'=2,'expert'=4] {'seq'}, dimensions={0}, use_global_device_ids=true | all-gather | bytes 49152 | tf_op jit(solution)/shard_map/all_gather | solution.py:12
  21.8 4.3 %all-gather.2 = f32[8,2,4]{2,1,0:T(2,128)S(1)} all-gather(f32[4,2,4]{2,1,0:T(2,128)S(1)} %fusion.44), channel_id=4, replica_groups=mesh['group'=4,'seq'=2,'expert'=4] {'seq'}, dimensions={0}, use_global_device_ids=true | all-gather | bytes 384 | tf_op jit(solution)/shard_map/all_gather | solution.py:12
  26.2 0.1 fusion.43
  26.3 2.8 %fusion.65 = f32[4,2048]{1,0:T(4,128)S(1)} fusion(bf16[4,1024]{1,0:T(4,128)(2,1)S(1)} %reshape.183, bf16[1024,2048]{1,0:T(8,128)(2,1)} %param.18), kind=kOutput, calls=%fused_computation.72 | convolution fusion | flops 16777216 | bytes 4235264 | tf_op jit(solution)/shard_map/dot_general | solution.py:76
  29.2 10.3 %psum.14 = f32[4,2048]{1,0:T(4,128)S(1)} all-reduce(f32[4,2048]{1,0:T(4,128)S(1)} %fusion.65), channel_id=1, replica_groups=mesh['group'=4,'seq'=2,'expert'=4] {'group'}, use_global_device_ids=true, to_apply=%region_2.3 | all-reduce | flops 8192 | bytes 65536 | tf_op jit(solution)/shard_map/psum | solution.py:77
  39.5 0.9 select_reduce_fusion
  40.4 0.7 convert_add_fusion
  41.1 4.6 %all_gather.27 = f32[4,4096]{1,0:T(4,128)S(1)} all-gather(f32[4,2048]{1,0:T(4,128)S(1)} %convert_add_fusion), channel_id=1, replica_groups=mesh['group'=4,'seq'=2,'expert'=4] {'seq'}, dimensions={1}, use_global_device_ids=true | all-gather | bytes 98304 | tf_op jit(solution)/shard_map/all_gather | solution.py:79
  45.7 0.7 convert_element_type.66
  46.4 0.1 multiply_reduce_fusion
  46.6 0.1 multiply_convert_fusion
  46.7 0.1 multiply_reduce_fusion.1
  46.7 0.2 convolution_convert_fusion
  47.0 0.8 copy.42
  47.7 5.4 %all-to-all-start = ((bf16[4,2,2,4096]{3,2,1,0:T(2,128)(2,1)}), bf16[4,2,2,4096]{3,2,1,0:T(2,128)(2,1)S(1)}, u32[]{:S(2)}, u32[]{:S(2)}) async-start(bf16[4,2,2,4096]{3,2,1,0:T(2,128)(2,1)} %bitcast.2), calls=%async_computation | async-start | bytes 262144 | tf_op jit(solution)/shard_map/all_to_all | solution.py:106
  53.1 0.0 all-reduce.2.cloned.1.call-start
  53.1 1.0 fusion.66
  54.1 0.9 multiply_reduce_fusion.2
  55.0 4.0 %all-to-all-done = bf16[4,2,2,4096]{3,2,1,0:T(2,128)(2,1)S(1)} async-done(((bf16[4,2,2,4096]{3,2,1,0:T(2,128)(2,1)}), bf16[4,2,2,4096]{3,2,1,0:T(2,128)(2,1)S(1)}, u32[]{:S(2)}, u32[]{:S(2)}) %all-to-all-start) | async-done | bytes 131104 | tf_op jit(solution)/shard_map/all_to_all | solution.py:106
  59.1 11.6 %fusion.12 = f32[4,2,2,1792]{3,0,2,1:T(4,128)S(1)} fusion(bf16[2,4096,1792]{2,1,0:T(8,128)(2,1)} %param.23, bf16[4,2,2,4096]{3,2,1,0:T(2,128)(2,1)S(1)} %all-to-all-done), kind=kOutput, calls=%fused_computation.9 | convolution fusion | flops 234881024 | bytes 29605888 | tf_op jit(solution)/shard_map/secd,edf->secf/dot_general | solution.py:107
  70.6 21.8 %fusion.9 = bf16[4,2,2,4096]{3,0,2,1:T(4,128)(2,1)} fusion(bf16[2,1792,4096]{2,1,0:T(8,128)(2,1)} %param.25, bf16[2,4096,1792]{2,1,0:T(8,128)(2,1)} %param.24, f32[4,2,2,1792]{3,0,2,1:T(4,128)S(1)} %fusion.12, bf16[4,2,2,4096]{3,2,1,0:T(2,128)(2,1)S(1)} %all-to-all-done), kind=kOutput, calls=%fused_computation.8 | convolution fusion | flops 469999616 | bytes 59097088 | tf_op jit(solution)/shard_map/secf,efd->secd/dot_general | solution.py:110
  92.4 0.0 all-reduce.2.cloned.1.call-update
  92.5 52.7 %all-reduce.2.cloned.1.call-done = bf16[4,2,2,4096]{3,0,2,1:T(4,128)(2,1)} async-done(((bf16[4,2,2,4096]{3,0,2,1:T(4,128)(2,1)}), bf16[4,2,2,4096]{3,0,2,1:T(4,128)(2,1)}) %all-reduce.2.cloned.1.call-update) | async-done | bytes 131088 | tf_op jit(solution)/shard_map/psum | solution.py:111
  145.2 0.9 convert_convert_fusion
  146.1 0.7 copy.37
  146.8 4.6 %all-to-all-start.1 = ((bf16[4,2,2,2048]{3,2,1,0:T(2,128)(2,1)}), bf16[4,2,2,2048]{3,2,1,0:T(2,128)(2,1)S(1)}, u32[]{:S(2)}, u32[]{:S(2)}) async-start(bf16[4,2,2,2048]{3,2,1,0:T(2,128)(2,1)} %copy.37), calls=%async_computation.1 | async-start | bytes 131072 | tf_op jit(solution)/shard_map/all_to_all | solution.py:114
  151.4 0.1 fusion.48
  151.5 5.7 %all-to-all-done.1 = bf16[4,2,2,2048]{3,2,1,0:T(2,128)(2,1)S(1)} async-done(((bf16[4,2,2,2048]{3,2,1,0:T(2,128)(2,1)}), bf16[4,2,2,2048]{3,2,1,0:T(2,128)(2,1)S(1)}, u32[]{:S(2)}, u32[]{:S(2)}) %all-to-all-start.1) | async-done | bytes 65568 | tf_op jit(solution)/shard_map/all_to_all | solution.py:114
  157.1 0.8 fusion.27
  (10 shorter events, 0.1 us)
Async XLA Ops:
  6.5 3.2 %copy-start = (bf16[4,128,2,128]{3,2,1,0:T(2,128)(2,1)S(1)}, bf16[4,128,2,128]{3,2,1,0:T(2,128)(2,1)}, u32[]{:S(2)}) copy-start(bf16[4,128,2,128]{3,2,1,0:T(2,128)(2,1)} %param.14) | copy-start | bytes 786436
  47.7 11.3 %all-to-all-start = ((bf16[4,2,2,4096]{3,2,1,0:T(2,128)(2,1)}), bf16[4,2,2,4096]{3,2,1,0:T(2,128)(2,1)S(1)}, u32[]{:S(2)}, u32[]{:S(2)}) async-start(bf16[4,2,2,4096]{3,2,1,0:T(2,128)(2,1)} %bitcast.2), calls=%async_computation | async-start | bytes 262144 | tf_op jit(solution)/shard_map/all_to_all | solution.py:106
  53.1 92.1 %all-reduce.2.cloned.1.call-start = ((), (), s32[]{:S(2)}) async-start(), calls=%async_computation.2 | async-start | bytes 262144 | tf_op jit(solution)/shard_map/psum | solution.py:111
  146.8 10.3 %all-to-all-start.1 = ((bf16[4,2,2,2048]{3,2,1,0:T(2,128)(2,1)}), bf16[4,2,2,2048]{3,2,1,0:T(2,128)(2,1)S(1)}, u32[]{:S(2)}, u32[]{:S(2)}) async-start(bf16[4,2,2,2048]{3,2,1,0:T(2,128)(2,1)} %copy.37), calls=%async_computation.1 | async-start | bytes 131072 | tf_op jit(solution)/shard_map/all_to_all | solution.py:114
Sparse Core Ops, SparseCore 0:
  92.6 52.6 all-reduce.1
where the time goes:
time: 166 us; the launch traced here: 165 us
  waiting for transfers between devices  62.5 us (38%)
  matrix products  40.5 us (24%)
  blocking collectives  28.9 us (17%)
  between operations  13.5 us (8%)
  starting transfers between devices  9.99 us (6%)
  other arithmetic  7.8 us (5%)
  local copies, waits for them, and re-layouts  1.72 us (1%)
    psum x1, waiting for transfers between devices, shards(): lax.psum(down_terms.astype(jnp.bfloat16), ('group', 'seq'))  52.7 us
    dot_general x1, matrix products, shards(): jnp.einsum('secf,efd->secd', activated, w_down, preferred_element_type=jn...  21.8 us
    all_gather x3, blocking collectives, combined_all(): everything = jax.tree.map(lambda part: lax.all_gather(part, axis), value)  14.1 us
    dot_general x1, matrix products, shards(): jnp.einsum('secd,edf->secf', inbound, w_gate, preferred_element_type=jnp....  11.6 us
    psum x1, blocking collectives, shards(): attention = lax.psum(partial_value, 'group')  10.3 us
    all_to_all x1, waiting for transfers between devices, shards(): lax.all_to_all(my_cols.astype(jnp.bfloat16), 'expert', split_axis=0, conc...  5.66 us
    all_to_all x1, starting transfers between devices, shards(): lax.all_to_all(outbound, 'expert', split_axis=0, concat_axis=0, tiled=True)  5.39 us
    all_to_all x1, starting transfers between devices, shards(): lax.all_to_all(my_cols.astype(jnp.bfloat16), 'expert', split_axis=0, conc...  4.59 us
  transfers between devices with their start and end apart: 3, of which 3 were waited for; matrix products, arithmetic and copies ran while one was open for 1% of the time, Pallas kernels for 0%

commit v1 on v0

--- a/solution.py
+++ b/solution.py
@@ -74,7 +74,14 @@
         .reshape(batch_rows, local_heads * head_dim)
     )
     partial_value = jnp.dot(attended, out_proj, preferred_element_type=jnp.float32)
-    attention = lax.psum(partial_value, "group")
+    attention = partial_value
+    wide_n = jax.lax.axis_size("group")
+    for rr in [nth for nth in (1, 2, 4, 8, 16) if nth < wide_n]:
+        fields = []
+        for idx in range(wide_n):
+            fields.append((idx, idx ^ rr))
+        shaped = jax.lax.ppermute(attention, axis_name="group", perm=fields)
+        attention = attention + shaped
     hidden = residual.astype(jnp.float32) + attention
     full_rows = lax.all_gather(hidden, "seq", axis=1, tiled=True)
     meansq = jnp.mean(full_rows * full_rows, axis=-1, keepdims=True)

time: 166 us -> 159 us (0.958)
  blocking collectives: 28.9 us -> 18.7 us
  waiting for transfers between devices: 62.5 us -> 64.6 us
  starting transfers between devices: 9.99 us -> 11.9 us
    psum x1 -> x0, blocking collectives: 10.3 us -> none  [shards(): attention = lax.psum(partial_value, 'group')]
    ppermute x0 -> x2, starting transfers between devices: none -> 2.08 us  [shards(): shaped = jax.lax.ppermute(attention, axis_name='group', perm=fields)]
  transfers between devices with their start and end apart: 3 -> 5, of which waited for: 3 -> 4; matrix products, arithmetic and copies ran while one was open for 1% -> 3% of each run, Pallas kernels for 0% -> 0%
where the time goes in v1:
time: 159 us
  waiting for transfers between devices  64.6 us (41%)
  matrix products  40.5 us (25%)
  blocking collectives  18.7 us (12%)
  between operations  13.5 us (8%)
  starting transfers between devices  11.9 us (7%)
  other arithmetic  7.79 us (5%)
  local copies, waits for them, and re-layouts  1.72 us (1%)
    psum x1, waiting for transfers between devices, shards(): lax.psum(down_terms.astype(jnp.bfloat16), ('group', 'seq'))  52.6 us
    dot_general x1, matrix products, shards(): jnp.einsum('secf,efd->secd', activated, w_down, preferred_element_type=jn...  21.8 us
    all_gather x3, blocking collectives, combined_all(): everything = jax.tree.map(lambda part: lax.all_gather(part, axis), value)  14.1 us
    dot_general x1, matrix products, shards(): jnp.einsum('secd,edf->secf', inbound, w_gate, preferred_element_type=jnp....  11.6 us
    all_to_all x1, waiting for transfers between devices, shards(): lax.all_to_all(my_cols.astype(jnp.bfloat16), 'expert', split_axis=0, conc...  5.66 us
    all_to_all x1, starting transfers between devices, shards(): lax.all_to_all(outbound, 'expert', split_axis=0, concat_axis=0, tiled=True)  5.23 us
    all_to_all x1, waiting for transfers between devices, shards(): lax.all_to_all(outbound, 'expert', split_axis=0, concat_axis=0, tiled=True)  5.03 us
    all_to_all x1, starting transfers between devices, shards(): lax.all_to_all(my_cols.astype(jnp.bfloat16), 'expert', split_axis=0, conc...  4.59 us
  transfers between devices with their start and end apart: 5, of which 4 were waited for; matrix products, arithmetic and copies ran while one was open for 3% of the time, Pallas kernels for 0%

profile of v1, /device:TPU:0, one launch (start us, length us, event | category | flops | bytes accessed | tf_op | source)
XLA Modules:
  0.0 158.6 jit_solution(14023852185957612089)
XLA Ops:
  6.5 0.0 copy-start
  6.5 0.7 broadcast_multiply_fusion
  7.3 0.1 add.74
  7.3 0.1 add.75
  7.4 0.1 add.77
  7.5 0.7 add_compare_fusion
  8.2 0.0 copy-done
  8.2 1.0 fusion.64
  9.3 5.3 %all-gather.1 = f32[8,2,4]{2,1,0:T(2,128)S(1)} all-gather(f32[4,2,4]{2,1,0:T(2,128)S(1)} %get-tuple-element.22), channel_id=3, replica_groups=mesh['group'=4,'seq'=2,'expert'=4] {'seq'}, dimensions={0}, use_global_device_ids=true | all-gather | bytes 384 | tf_op jit(solution)/shard_map/all_gather | solution.py:12
  14.6 0.2 fusion.44
  14.7 1.2 fusion.29
  15.9 4.4 %all-gather = f32[8,2,4,128]{3,2,1,0:T(4,128)S(1)} all-gather(f32[4,2,4,128]{3,2,1,0:T(4,128)S(1)} %fusion.29), channel_id=2, replica_groups=mesh['group'=4,'seq'=2,'expert'=4] {'seq'}, dimensions={0}, use_global_device_ids=true | all-gather | bytes 49152 | tf_op jit(solution)/shard_map/all_gather | solution.py:12
  20.3 4.3 %all-gather.2 = f32[8,2,4]{2,1,0:T(2,128)S(1)} all-gather(f32[4,2,4]{2,1,0:T(2,128)S(1)} %fusion.44), channel_id=4, replica_groups=mesh['group'=4,'seq'=2,'expert'=4] {'seq'}, dimensions={0}, use_global_device_ids=true | all-gather | bytes 384 | tf_op jit(solution)/shard_map/all_gather | solution.py:12
  24.7 0.1 fusion.43
  24.8 2.8 %fusion.65 = f32[4,2048]{1,0:T(4,128)S(1)} fusion(bf16[4,1024]{1,0:T(4,128)(2,1)S(1)} %reshape.183, bf16[1024,2048]{1,0:T(8,128)(2,1)} %param.18), kind=kOutput, calls=%fused_computation.72 | convolution fusion | flops 16777216 | bytes 4235264 | tf_op jit(solution)/shard_map/dot_general | solution.py:76
  27.7 0.0 collective-permute-start
  27.7 0.8 fusion.56
  28.4 0.7 fusion.55
  29.2 0.9 select_reduce_fusion
  30.1 0.0 collective-permute-done
  30.1 2.1 %collective-permute-start.1 = (f32[4,2048]{1,0:T(4,128)S(1)}, f32[4,2048]{1,0:T(4,128)S(1)}, u32[]{:S(2)}, u32[]{:S(2)}) collective-permute-start(f32[4,2048]{1,0:T(4,128)S(1)} %add.82), channel_id=1, source_target_pairs={{0,16},{8,24},{16,0},{24,8},{1,17},{9,25},{17,1},{25,9},{2,18},{10... | collective-permute-start | bytes 98312 | tf_op jit(solution)/shard_map/ppermute | solution.py:83
  32.2 0.1 multiply_reduce_fusion.1
  32.3 0.7 convert_element_type.66
  33.0 1.3 collective-permute-done.1
  34.3 0.7 add_add_fusion
  35.0 4.6 %all_gather.27 = f32[4,4096]{1,0:T(4,128)S(1)} all-gather(f32[4,2048]{1,0:T(4,128)S(1)} %add_add_fusion), channel_id=1, replica_groups=mesh['group'=4,'seq'=2,'expert'=4] {'seq'}, dimensions={1}, use_global_device_ids=true | all-gather | bytes 98304 | tf_op jit(solution)/shard_map/all_gather | solution.py:86
  39.6 0.1 multiply_reduce_fusion
  39.8 0.1 multiply_convert_fusion
  39.9 1.0 fusion.66
  40.8 0.2 convolution_convert_fusion
  41.1 0.8 copy.42
  41.9 5.2 %all-to-all-start = ((bf16[4,2,2,4096]{3,2,1,0:T(2,128)(2,1)}), bf16[4,2,2,4096]{3,2,1,0:T(2,128)(2,1)S(1)}, u32[]{:S(2)}, u32[]{:S(2)}) async-start(bf16[4,2,2,4096]{3,2,1,0:T(2,128)(2,1)} %bitcast.2), calls=%async_computation | async-start | bytes 262144 | tf_op jit(solution)/shard_map/all_to_all | solution.py:113
  47.1 0.0 all-reduce.2.cloned.1.call-start
  47.1 0.8 multiply_reduce_fusion.2
  48.0 5.0 %all-to-all-done = bf16[4,2,2,4096]{3,2,1,0:T(2,128)(2,1)S(1)} async-done(((bf16[4,2,2,4096]{3,2,1,0:T(2,128)(2,1)}), bf16[4,2,2,4096]{3,2,1,0:T(2,128)(2,1)S(1)}, u32[]{:S(2)}, u32[]{:S(2)}) %all-to-all-start) | async-done | bytes 131104 | tf_op jit(solution)/shard_map/all_to_all | solution.py:113
  53.0 11.6 %fusion.12 = f32[4,2,2,1792]{3,0,2,1:T(4,128)S(1)} fusion(bf16[2,4096,1792]{2,1,0:T(8,128)(2,1)} %param.23, bf16[4,2,2,4096]{3,2,1,0:T(2,128)(2,1)S(1)} %all-to-all-done), kind=kOutput, calls=%fused_computation.9 | convolution fusion | flops 234881024 | bytes 29605888 | tf_op jit(solution)/shard_map/secd,edf->secf/dot_general | solution.py:114
  64.6 21.8 %fusion.9 = bf16[4,2,2,4096]{3,0,2,1:T(4,128)(2,1)} fusion(bf16[2,1792,4096]{2,1,0:T(8,128)(2,1)} %param.25, bf16[2,4096,1792]{2,1,0:T(8,128)(2,1)} %param.24, f32[4,2,2,1792]{3,0,2,1:T(4,128)S(1)} %fusion.12, bf16[4,2,2,4096]{3,2,1,0:T(2,128)(2,1)S(1)} %all-to-all-done), kind=kOutput, calls=%fused_computation.8 | convolution fusion | flops 469999616 | bytes 59097088 | tf_op jit(solution)/shard_map/secf,efd->secd/dot_general | solution.py:117
  86.4 0.0 all-reduce.2.cloned.1.call-update
  86.4 52.6 %all-reduce.2.cloned.1.call-done = bf16[4,2,2,4096]{3,0,2,1:T(4,128)(2,1)} async-done(((bf16[4,2,2,4096]{3,0,2,1:T(4,128)(2,1)}), bf16[4,2,2,4096]{3,0,2,1:T(4,128)(2,1)}) %all-reduce.2.cloned.1.call-update) | async-done | bytes 131088 | tf_op jit(solution)/shard_map/psum | solution.py:118
  139.1 0.9 convert_convert_fusion
  139.9 0.7 copy.37
  140.6 4.6 %all-to-all-start.1 = ((bf16[4,2,2,2048]{3,2,1,0:T(2,128)(2,1)}), bf16[4,2,2,2048]{3,2,1,0:T(2,128)(2,1)S(1)}, u32[]{:S(2)}, u32[]{:S(2)}) async-start(bf16[4,2,2,2048]{3,2,1,0:T(2,128)(2,1)} %copy.37), calls=%async_computation.1 | async-start | bytes 131072 | tf_op jit(solution)/shard_map/all_to_all | solution.py:121
  145.2 0.1 fusion.48
  145.3 5.7 %all-to-all-done.1 = bf16[4,2,2,2048]{3,2,1,0:T(2,128)(2,1)S(1)} async-done(((bf16[4,2,2,2048]{3,2,1,0:T(2,128)(2,1)}), bf16[4,2,2,2048]{3,2,1,0:T(2,128)(2,1)S(1)}, u32[]{:S(2)}, u32[]{:S(2)}) %all-to-all-start.1) | async-done | bytes 65568 | tf_op jit(solution)/shard_map/all_to_all | solution.py:121
  151.0 0.8 fusion.27
  (11 shorter events, 0.2 us)
Async XLA Ops:
  6.5 1.7 %copy-start = (bf16[4,128,2,128]{3,2,1,0:T(2,128)(2,1)S(1)}, bf16[4,128,2,128]{3,2,1,0:T(2,128)(2,1)}, u32[]{:S(2)}) copy-start(bf16[4,128,2,128]{3,2,1,0:T(2,128)(2,1)} %param.14) | copy-start | bytes 786436
  27.7 2.5 %collective-permute-start = (f32[4,2048]{1,0:T(4,128)S(1)}, f32[4,2048]{1,0:T(4,128)S(1)}, u32[]{:S(2)}, u32[]{:S(2)}) collective-permute-start(f32[4,2048]{1,0:T(4,128)S(1)} %fusion.65), channel_id=1, source_target_pairs={{0,8},{8,0},{16,24},{24,16},{1,9},{9,1},{17,25},{25,17},{2,10},{10... | collective-permute-start | bytes 98312 | tf_op jit(solution)/shard_map/ppermute | solution.py:83
  30.1 4.1 %collective-permute-start.1 = (f32[4,2048]{1,0:T(4,128)S(1)}, f32[4,2048]{1,0:T(4,128)S(1)}, u32[]{:S(2)}, u32[]{:S(2)}) collective-permute-start(f32[4,2048]{1,0:T(4,128)S(1)} %add.82), channel_id=1, source_target_pairs={{0,16},{8,24},{16,0},{24,8},{1,17},{9,25},{17,1},{25,9},{2,18},{10... | collective-permute-start | bytes 98312 | tf_op jit(solution)/shard_map/ppermute | solution.py:83
  41.9 11.2 %all-to-all-start = ((bf16[4,2,2,4096]{3,2,1,0:T(2,128)(2,1)}), bf16[4,2,2,4096]{3,2,1,0:T(2,128)(2,1)S(1)}, u32[]{:S(2)}, u32[]{:S(2)}) async-start(bf16[4,2,2,4096]{3,2,1,0:T(2,128)(2,1)} %bitcast.2), calls=%async_computation | async-start | bytes 262144 | tf_op jit(solution)/shard_map/all_to_all | solution.py:113
  47.1 92.0 %all-reduce.2.cloned.1.call-start = ((), (), s32[]{:S(2)}) async-start(), calls=%async_computation.2 | async-start | bytes 262144 | tf_op jit(solution)/shard_map/psum | solution.py:118
  140.6 10.3 %all-to-all-start.1 = ((bf16[4,2,2,2048]{3,2,1,0:T(2,128)(2,1)}), bf16[4,2,2,2048]{3,2,1,0:T(2,128)(2,1)S(1)}, u32[]{:S(2)}, u32[]{:S(2)}) async-start(bf16[4,2,2,2048]{3,2,1,0:T(2,128)(2,1)} %copy.37), calls=%async_computation.1 | async-start | bytes 131072 | tf_op jit(solution)/shard_map/all_to_all | solution.py:121
Sparse Core Ops, SparseCore 0:
  86.6 52.4 all-reduce.1
